TPU v7x, 32 devices: a whole 2x2x4 slice. The times are simulated.
32 devices in a mesh: seq: 8 (over z, y), head: 4 (over x, core).
Axes of the slice: x: 2, y: 2, z: 4, core: 2. Of those that a mesh axis runs over, the one named last changes fastest.
Arguments:
- hidden: bfloat16 [4096, 8192], P('seq', 'head'), may hold values from -6 to 6
- gain: float32 [8192], replicated, may hold values from 0.25 to 1.75
- key_matrix: bfloat16 [8192, 512], P(None, 'head'), may hold values from -0.0625 to 0.0625
- value_matrix: bfloat16 [8192, 512], P(None, 'head'), may hold values from -0.0625 to 0.0625
- queries: bfloat16 [64, 4096], P(None, 'head'), may hold values from -360 to 360
- window_len: int32 [4], P('head'), may hold values from 16 to 64, as said below
- kernel_width: int32 [4], P('head'), may hold values from 1 to 15, as said below
- kept_block_count: int32 [4], P('head'), may hold values from 1 to 16
Outputs:
- block_scores: float32 [4, 32], P('head', 'seq')
- kept_fraction: float32 [4], P('head')
Inputs may be any that keep to these rules, and one draw needn't show every extreme that they name: `window_len`: at least one key-value head uses all 64 window queries. `kernel_width`: odd; at least one key-value head has width 15.
All inputs are finite; a program needn't handle non-finite values.
Results may differ from a plain program's by a relative error of at most 0.0112.
The roundings to bfloat16 on the way count: a program that leaves them out, or rounds other values in their place, can miss the bound.
Values may be sent and summed in bfloat16 or wider, within the bound.
No kernel may reach another device: no remote copies, remote signals or barrier semaphores. Data moves between devices by JAX's collectives and lax.ppermute only.
A program may use at most 128 MiB of HBM per device.

v0:
```python
import jax
import jax.numpy as jnp
from jax import lax
from jax.sharding import PartitionSpec as P

BLK = 128
KERNEL_LIMIT = 15


def with_halo(x, sides, width):
    for axis, dim in sides:
        count, length = (lax.axis_size(axis), x.shape[dim])
        up = [(i, (i + 1) % count) for i in range(count - 1)]
        down = [(j, i) for i, j in up]
        last = lax.slice_in_dim(x, length - width, length, axis=dim)
        leading = lax.slice_in_dim(x, 0, width, axis=dim)
        before = lax.ppermute(last, axis, up)
        after = lax.ppermute(leading, axis, down)
        x = jnp.concatenate([before, x, after], axis=dim)
    return x


def rotate(raw, positions):
    half = raw.shape[1] // 2
    freq = 500000.0 ** (-(jnp.arange(half).astype(jnp.float32) * 2.0) / raw.shape[1])
    angle = positions[:, None] * freq[None, :]
    leading_part = raw[:, :half]
    trailing_part = raw[:, half:]
    return jnp.concatenate(
        [
            leading_part * jnp.cos(angle) - trailing_part * jnp.sin(angle),
            trailing_part * jnp.cos(angle) + leading_part * jnp.sin(angle),
        ],
        axis=1,
    )


def local(
    hidden, gain, key_matrix, value_matrix, queries, window_len, kernel_width, kept_block_count
):
    tok_rows = hidden.shape[0]
    full_width = gain.shape[0]
    head_size = key_matrix.shape[1]
    floats = hidden.astype(jnp.float32)
    sumsq = lax.psum(jnp.sum(floats * floats, axis=1), "head")
    inv_rms = lax.rsqrt(sumsq / full_width + 1e-05)
    joined = jnp.concatenate([key_matrix, value_matrix], axis=1)
    normed = (
        lax.all_gather(hidden, "head", axis=1, tiled=True).astype(jnp.float32) * gain[None, :]
    ).astype(jnp.bfloat16)
    projected = jnp.dot(normed, joined, preferred_element_type=jnp.float32)
    projected = projected * inv_rms[:, None]
    tok_index = lax.axis_index("seq") * tok_rows + jnp.arange(tok_rows)
    positions = tok_index.astype(jnp.float32)
    keys = rotate(projected[:, :head_size], positions).astype(jnp.bfloat16)
    vmag = jnp.mean(jnp.abs(projected[:, head_size:]), axis=1)
    window = queries.shape[0]
    group_heads = queries.shape[1] // head_size
    query_rows = queries.reshape(window * group_heads, head_size)
    scores = lax.dot_general(
        query_rows, keys, (((1,), (1,)), ((), ())), preferred_element_type=jnp.float32
    ) * head_size ** (-0.5)
    total_tokens = tok_rows * lax.axis_size("seq")
    limit = jnp.repeat(total_tokens - window + jnp.arange(window), group_heads)
    allowed = tok_index[None, :] <= limit[:, None]
    scores = jnp.where(allowed, scores, jnp.float32(-1e30))
    local_top = jnp.max(scores, axis=1)
    row_top = lax.pmax(local_top, "seq")
    expo = jnp.exp(scores - row_top[:, None])
    row_total = lax.psum(jnp.sum(expo, axis=1), "seq")
    rescale = jnp.ones_like(row_total)
    used = (jnp.arange(window) >= window - window_len[0]).astype(jnp.float32)
    row_weight = jnp.repeat(used, group_heads) * rescale / row_total
    column = jnp.dot(row_weight, expo, precision=lax.Precision.HIGHEST) * vmag
    reach = (KERNEL_LIMIT - 1) // 2
    padded = with_halo(column, (("seq", 0),), reach)
    kernel_halfspan = (kernel_width[0] - 1) // 2
    pooled = column
    for shift in range(1, reach + 1):
        wider = jnp.maximum(
            jnp.maximum(pooled, padded[reach + shift : reach + shift + tok_rows]),
            padded[reach - shift : reach - shift + tok_rows],
        )
        pooled = jnp.where(shift <= kernel_halfspan, wider, pooled)
    local_blocks = jnp.sum(pooled.reshape(tok_rows // BLK, BLK), axis=1)[None, :]
    everything = lax.all_gather(local_blocks, "seq", axis=1, tiled=True)[0]
    ordered = -jnp.sort(-everything)
    ranks = jnp.arange(ordered.shape[0])
    kept = jnp.sum(jnp.where(ranks < kept_block_count[0], ordered, jnp.float32(0.0)))
    fraction = (kept / jnp.sum(ordered)).reshape(1)
    return (local_blocks, fraction)


def solution(mesh):
    return jax.shard_map(
        local,
        mesh=mesh,
        in_specs=(
            P("seq", "head"),
            P(),
            P(None, "head"),
            P(None, "head"),
            P(None, "head"),
            P("head"),
            P("head"),
            P("head"),
        ),
        out_specs=(P("head", "seq"), P("head")),
        check_vma=False,
    )
```

profile of v0, /device:TPU:0, one launch (start us, length us, event | category | flops | bytes accessed | tf_op | source)
XLA Modules:
  0.0 157.1 jit_solution(7609627779435552544)
XLA Ops:
  7.2 0.0 copy-start.1
  7.2 0.0 copy-start.2
  7.2 0.0 all-gather.3.cloned.1.call-start
  7.2 0.7 all-gather.3.cloned.1.call-update
  8.6 1.0 reshape.43
  9.6 0.1 broadcast_in_dim.24
  9.6 0.1 le.16
  10.4 0.1 broadcast_in_dim.23
  10.5 0.1 reshape.42
  11.3 1.2 dynamic-slice
  13.1 2.1 %multiply_reduce_fusion = f32[512]{0:T(512)S(1)} fusion(bf16[512,2048]{1,0:T(8,128)(2,1)} %param.8), kind=kLoop, calls=%fused_computation.6 | loop fusion | flops 3145216 | bytes 2099200 | tf_op jit(solution)/shard_map/reduce_sum | solution.py:45
  15.2 8.4 %psum.14 = f32[512]{0:T(512)S(1)} all-reduce(f32[512]{0:T(512)S(1)} %multiply_reduce_fusion), channel_id=1, replica_groups=mesh['seq'=8,'head'=4] {'head'}, use_global_device_ids=true, to_apply=%region_1.0 | all-reduce | flops 512 | bytes 4096 | tf_op jit(solution)/shard_map/psum | solution.py:45
  23.6 46.9 %all-gather.3.cloned.1.call-done = bf16[512,8192]{1,0:T(8,128)(2,1)} async-done(((bf16[512,2048]{1,0:T(8,128)(2,1)}), bf16[512,8192]{1,0:T(8,128)(2,1)}) %all-gather.3.cloned.1.call-update) | async-done | bytes 8388624 | tf_op jit(solution)/shard_map/all_gather | solution.py:49
  70.6 0.0 copy-done.1
  70.6 0.0 copy-done.2
  70.6 6.3 %fusion.7 = f32[512,256]{0,1:T(8,128)S(1)} fusion(bf16[8192,128]{1,0:T(8,128)(2,1)S(1)} %copy-done.1, bf16[8192,128]{1,0:T(8,128)(2,1)} %param.10, bf16[512,8192]{1,0:T(8,128)(2,1)} %all-gather.3.cloned.1.call-done, f32[8192]{0:T(1024)S(1)} %copy-done.2, f32[512]{0:T(512)S(1)} %add_rsqrt_fusion), kind=kOutput, calls=%fused_computation.10 | convolution fusion | flops 2168586240 | bytes 13142016 | tf_op jit(solution)/shard_map/dot_general | solution.py:51
  77.0 0.6 fusion.19
  77.5 0.4 fusion.31
  77.9 21.4 %pmax.7 = f32[512]{0:T(512)S(1)} all-reduce(f32[512]{0:T(512)S(1)} %get-tuple-element.13), channel_id=1, replica_groups=mesh['seq'=8,'head'=4] {'seq'}, use_global_device_ids=true, to_apply=%region_3.4 | all-reduce | flops 512 | bytes 4096 | tf_op jit(solution)/shard_map/pmax | solution.py:68
  99.3 0.2 fusion.11
  99.5 17.1 %psum.15 = f32[512]{0:T(512)S(1)} all-reduce(f32[512]{0:T(512)S(1)} %fusion.11), channel_id=1, replica_groups=mesh['seq'=8,'head'=4] {'seq'}, use_global_device_ids=true, to_apply=%region_5.6 | all-reduce | flops 512 | bytes 4096 | tf_op jit(solution)/shard_map/psum | solution.py:70
  116.6 1.0 fusion.10
  117.6 0.1 fusion.30
  117.7 1.3 collective-permute-start
  119.0 4.5 %collective-permute-start.1 = (f32[7]{0:T(128)S(1)}, f32[7]{0:T(128)S(1)}, u32[]{:S(2)}, u32[]{:S(2)}) collective-permute-start(f32[7]{0:T(128)S(1)} %get-tuple-element.12), channel_id=1, source_target_pairs={{0,4},{4,8},{8,12},{12,16},{16,20},{20,24},{24,28},{1,5},{5,9},{9,... | collective-permute-start | bytes 92 | tf_op jit(solution)/shard_map/ppermute | solution.py:17
  123.6 0.0 collective-permute-done
  123.6 1.3 collective-permute-done.1
  124.8 0.1 pad_maximum_fusion
  124.9 0.2 bitcast_reduce_fusion
  125.1 0.0 copy-start
  125.1 0.2 dynamic-update-slice
  125.4 20.0 %all-reduce = f32[32]{0:T(128)S(1)} all-reduce(f32[32]{0:T(128)S(1)} %dynamic-update-slice), channel_id=2, replica_groups=mesh['seq'=8,'head'=4] {'seq'}, use_global_device_ids=true, to_apply=%add | all-reduce | flops 32 | bytes 256
  145.4 1.6 %sort.15 = (f32[32]{0:T(128)S(1)}, s32[32]{0:T(128)}) sort(f32[32]{0:T(128)S(1)} %neg.23, s32[32]{0:T(128)S(1)} %iota.29), dimensions={0}, to_apply=%region_8.9 | sort | flops 160 | bytes 512 | tf_op jit(solution)/shard_map/jit(sort)/sort | solution.py:87
  147.0 0.7 fusion.29
  149.1 0.0 copy-done
  (12 shorter events, 0.1 us)
Async XLA Ops:
  7.2 63.4 %copy-start.1 = (bf16[8192,128]{1,0:T(8,128)(2,1)S(1)}, bf16[8192,128]{1,0:T(8,128)(2,1)}, u32[]{:S(2)}) copy-start(bf16[8192,128]{1,0:T(8,128)(2,1)} %param.11) | copy-start | bytes 6291460
  7.2 63.4 %copy-start.2 = (f32[8192]{0:T(1024)S(1)}, f32[8192]{0:T(1024)}, u32[]{:S(2)}) copy-start(f32[8192]{0:T(1024)} %param.9) | copy-start | bytes 98308
  7.2 63.4 %all-gather.3.cloned.1.call-start = ((), (), s32[]{:S(2)}) async-start(), calls=%async_computation | async-start | bytes 10485760 | tf_op jit(solution)/shard_map/all_gather | solution.py:49
  117.7 5.9 %collective-permute-start = (f32[7]{0:T(128)S(1)}, f32[7]{0:T(128)S(1)}, u32[]{:S(2)}, u32[]{:S(2)}) collective-permute-start(f32[7]{0:T(128)S(1)} %get-tuple-element.11), channel_id=1, source_target_pairs={{4,0},{8,4},{12,8},{16,12},{20,16},{24,20},{28,24},{5,1},{9,5},{13... | collective-permute-start | bytes 92 | tf_op jit(solution)/shard_map/ppermute | solution.py:18
  119.0 5.8 %collective-permute-start.1 = (f32[7]{0:T(128)S(1)}, f32[7]{0:T(128)S(1)}, u32[]{:S(2)}, u32[]{:S(2)}) collective-permute-start(f32[7]{0:T(128)S(1)} %get-tuple-element.12), channel_id=1, source_target_pairs={{0,4},{4,8},{8,12},{12,16},{16,20},{20,24},{24,28},{1,5},{5,9},{9,... | collective-permute-start | bytes 92 | tf_op jit(solution)/shard_map/ppermute | solution.py:17
  125.1 24.0 %copy-start = (f32[4]{0:T(128)}, f32[4]{0:T(128)S(1)}, u32[]{:S(2)}) copy-start(f32[4]{0:T(128)S(1)} %bitcast_reduce_fusion) | copy-start | bytes 52
Sparse Core Ops, SparseCore 0:
  9.6 60.9 all-gather.2
where the time goes:
time: 157 us
  blocking collectives  66.9 us (43%)
  waiting for transfers between devices  48.9 us (31%)
  between operations  19.3 us (12%)
  matrix products  7.68 us (5%)
  starting transfers between devices  5.88 us (4%)
  other arithmetic  5.53 us (4%)
  local copies, waits for them, and re-layouts  2.88 us (2%)
    all_gather x1, waiting for transfers between devices, local(): lax.all_gather(hidden, 'head', axis=1, tiled=True).astype(jnp.float32)  46.9 us
    pmax x1, blocking collectives, local(): row_top = lax.pmax(local_top, 'seq')  21.4 us
    unnamed x1, blocking collectives  20 us
    psum x1, blocking collectives, local(): row_total = lax.psum(jnp.sum(expo, axis=1), 'seq')  17.1 us
    psum x1, blocking collectives, local(): sumsq = lax.psum(jnp.sum(floats * floats, axis=1), 'head')  8.37 us
    dot_general x1, matrix products, local(): projected = jnp.dot(normed, joined, preferred_element_type=jnp.float32)  6.35 us
    ppermute x1, starting transfers between devices, with_halo(): before = lax.ppermute(last, axis, up)  4.55 us
  transfers between devices with their start and end apart: 3, of which 2 were waited for; matrix products, arithmetic and copies ran while one was open for 3% of the time, Pallas kernels for 0%

commit v1 on v0

--- a/solution.py
+++ b/solution.py
@@ -1,3 +1,4 @@
+import functools
 import jax
 import jax.numpy as jnp
 from jax import lax
@@ -5,6 +6,14 @@
 
 BLK = 128
 KERNEL_LIMIT = 15
+
+
+def guide_rails_up(view, axis_name):
+    local_next = lax.all_gather(view, axis_name)
+    return jnp.sum(local_next, axis=0)
+
+
+case_link = functools.partial(guide_rails_up, axis_name="seq")
 
 
 def with_halo(x, sides, width):
@@ -67,7 +76,7 @@
     local_top = jnp.max(scores, axis=1)
     row_top = lax.pmax(local_top, "seq")
     expo = jnp.exp(scores - row_top[:, None])
-    row_total = lax.psum(jnp.sum(expo, axis=1), "seq")
+    row_total = case_link(jnp.sum(expo, axis=1))
     rescale = jnp.ones_like(row_total)
     used = (jnp.arange(window) >= window - window_len[0]).astype(jnp.float32)
     row_weight = jnp.repeat(used, group_heads) * rescale / row_total

time: 157 us -> 166 us (1.057)
  blocking collectives: 66.9 us -> 75.3 us
    all_gather x0 -> x1, blocking collectives: none -> 26.1 us  [guide_rails_up(): local_next = lax.all_gather(view, axis_name)]
    psum x1 -> x0, blocking collectives: 17.1 us -> none  [local(): row_total = lax.psum(jnp.sum(expo, axis=1), 'seq')]
where the time goes in v1:
time: 166 us; the launch traced here: 165 us
  blocking collectives  75.3 us (45%)
  waiting for transfers between devices  48.9 us (29%)
  between operations  19.3 us (12%)
  matrix products  7.68 us (5%)
  starting transfers between devices  5.88 us (4%)
  other arithmetic  5.56 us (3%)
  local copies, waits for them, and re-layouts  2.88 us (2%)
    all_gather x1, waiting for transfers between devices, local(): lax.all_gather(hidden, 'head', axis=1, tiled=True).astype(jnp.float32)  46.9 us
    all_gather x1, blocking collectives, guide_rails_up(): local_next = lax.all_gather(view, axis_name)  26.1 us
    pmax x1, blocking collectives, local(): row_top = lax.pmax(local_top, 'seq')  21.4 us
    unnamed x1, blocking collectives  19.4 us
    psum x1, blocking collectives, local(): sumsq = lax.psum(jnp.sum(floats * floats, axis=1), 'head')  8.37 us
    dot_general x1, matrix products, local(): projected = jnp.dot(normed, joined, preferred_element_type=jnp.float32)  6.35 us
    ppermute x1, starting transfers between devices, with_halo(): before = lax.ppermute(last, axis, up)  4.55 us
  transfers between devices with their start and end apart: 3, of which 2 were waited for; matrix products, arithmetic and copies ran while one was open for 3% of the time, Pallas kernels for 0%

profile of v1, /device:TPU:0, one launch (start us, length us, event | category | flops | bytes accessed | tf_op | source)
XLA Modules:
  0.0 165.4 jit_solution(12819597643951956781)
XLA Ops:
  7.2 0.0 copy-start.1
  7.2 0.0 copy-start.2
  7.2 0.0 all-gather.5.cloned.1.call-start
  7.2 0.7 all-gather.5.cloned.1.call-update
  8.6 1.0 reshape.43
  9.6 0.1 broadcast_in_dim.24
  9.6 0.1 le.16
  10.4 0.1 broadcast_in_dim.23
  10.5 0.1 reshape.42
  11.3 1.2 dynamic-slice
  13.1 2.1 %multiply_reduce_fusion = f32[512]{0:T(512)S(1)} fusion(bf16[512,2048]{1,0:T(8,128)(2,1)} %param.8), kind=kLoop, calls=%fused_computation.6 | loop fusion | flops 3145216 | bytes 2099200 | tf_op jit(solution)/shard_map/reduce_sum | solution.py:54
  15.2 8.4 %psum.7 = f32[512]{0:T(512)S(1)} all-reduce(f32[512]{0:T(512)S(1)} %multiply_reduce_fusion), channel_id=1, replica_groups=mesh['seq'=8,'head'=4] {'head'}, use_global_device_ids=true, to_apply=%region_1.0 | all-reduce | flops 512 | bytes 4096 | tf_op jit(solution)/shard_map/psum | solution.py:54
  23.6 46.9 %all-gather.5.cloned.1.call-done = bf16[512,8192]{1,0:T(8,128)(2,1)} async-done(((bf16[512,2048]{1,0:T(8,128)(2,1)}), bf16[512,8192]{1,0:T(8,128)(2,1)}) %all-gather.5.cloned.1.call-update) | async-done | bytes 8388624 | tf_op jit(solution)/shard_map/all_gather | solution.py:58
  70.6 0.0 copy-done.1
  70.6 0.0 copy-done.2
  70.6 6.3 %fusion.7 = f32[512,256]{0,1:T(8,128)S(1)} fusion(bf16[8192,128]{1,0:T(8,128)(2,1)S(1)} %copy-done.1, bf16[8192,128]{1,0:T(8,128)(2,1)} %param.10, bf16[512,8192]{1,0:T(8,128)(2,1)} %all-gather.5.cloned.1.call-done, f32[8192]{0:T(1024)S(1)} %copy-done.2, f32[512]{0:T(512)S(1)} %add_rsqrt_fusion), kind=kOutput, calls=%fused_computation.10 | convolution fusion | flops 2168586240 | bytes 13142016 | tf_op jit(solution)/shard_map/dot_general | solution.py:60
  77.0 0.6 fusion.19
  77.5 0.4 fusion.31
  77.9 21.4 %pmax.7 = f32[512]{0:T(512)S(1)} all-reduce(f32[512]{0:T(512)S(1)} %get-tuple-element.13), channel_id=1, replica_groups=mesh['seq'=8,'head'=4] {'seq'}, use_global_device_ids=true, to_apply=%region_3.4 | all-reduce | flops 512 | bytes 4096 | tf_op jit(solution)/shard_map/pmax | solution.py:77
  99.3 0.2 fusion.11
  99.5 26.1 %all-gather.2 = f32[8,1,512]{2,1,0:T(1,128)S(1)} all-gather(f32[1,1,512]{2,1,0:T(1,128)S(1)} %bitcast.20), channel_id=2, replica_groups=mesh['seq'=8,'head'=4] {'seq'}, dimensions={0}, use_global_device_ids=true | all-gather | bytes 18432 | tf_op jit(solution)/shard_map/all_gather | solution.py:12
  125.7 1.0 fusion.10
  126.6 0.1 fusion.30
  126.7 1.3 collective-permute-start
  128.0 4.5 %collective-permute-start.1 = (f32[7]{0:T(128)S(1)}, f32[7]{0:T(128)S(1)}, u32[]{:S(2)}, u32[]{:S(2)}) collective-permute-start(f32[7]{0:T(128)S(1)} %get-tuple-element.12), channel_id=1, source_target_pairs={{0,4},{4,8},{8,12},{12,16},{16,20},{20,24},{24,28},{1,5},{5,9},{9,... | collective-permute-start | bytes 92 | tf_op jit(solution)/shard_map/ppermute | solution.py:26
  132.6 0.0 collective-permute-done
  132.6 1.3 collective-permute-done.1
  133.9 0.1 pad_maximum_fusion
  133.9 0.2 bitcast_reduce_fusion
  134.1 0.0 copy-start
  134.2 0.2 dynamic-update-slice
  134.4 19.4 %all-reduce = f32[32]{0:T(128)S(1)} all-reduce(f32[32]{0:T(128)S(1)} %dynamic-update-slice), channel_id=3, replica_groups=mesh['seq'=8,'head'=4] {'seq'}, use_global_device_ids=true, to_apply=%add | all-reduce | flops 32 | bytes 256
  153.8 1.6 sort.15
  155.4 0.7 fusion.29
  157.5 0.0 copy-done
  (13 shorter events, 0.1 us)
Async XLA Ops:
  7.2 63.4 %copy-start.1 = (bf16[8192,128]{1,0:T(8,128)(2,1)S(1)}, bf16[8192,128]{1,0:T(8,128)(2,1)}, u32[]{:S(2)}) copy-start(bf16[8192,128]{1,0:T(8,128)(2,1)} %param.11) | copy-start | bytes 6291460
  7.2 63.4 %copy-start.2 = (f32[8192]{0:T(1024)S(1)}, f32[8192]{0:T(1024)}, u32[]{:S(2)}) copy-start(f32[8192]{0:T(1024)} %param.9) | copy-start | bytes 98308
  7.2 63.4 %all-gather.5.cloned.1.call-start = ((), (), s32[]{:S(2)}) async-start(), calls=%async_computation | async-start | bytes 10485760 | tf_op jit(solution)/shard_map/all_gather | solution.py:58
  126.7 5.9 %collective-permute-start = (f32[7]{0:T(128)S(1)}, f32[7]{0:T(128)S(1)}, u32[]{:S(2)}, u32[]{:S(2)}) collective-permute-start(f32[7]{0:T(128)S(1)} %get-tuple-element.11), channel_id=1, source_target_pairs={{4,0},{8,4},{12,8},{16,12},{20,16},{24,20},{28,24},{5,1},{9,5},{13... | collective-permute-start | bytes 92 | tf_op jit(solution)/shard_map/ppermute | solution.py:27
  128.0 5.8 %collective-permute-start.1 = (f32[7]{0:T(128)S(1)}, f32[7]{0:T(128)S(1)}, u32[]{:S(2)}, u32[]{:S(2)}) collective-permute-start(f32[7]{0:T(128)S(1)} %get-tuple-element.12), channel_id=1, source_target_pairs={{0,4},{4,8},{8,12},{12,16},{16,20},{20,24},{24,28},{1,5},{5,9},{9,... | collective-permute-start | bytes 92 | tf_op jit(solution)/shard_map/ppermute | solution.py:26
  134.1 23.3 %copy-start = (f32[4]{0:T(128)}, f32[4]{0:T(128)S(1)}, u32[]{:S(2)}) copy-start(f32[4]{0:T(128)S(1)} %bitcast_reduce_fusion) | copy-start | bytes 52
Sparse Core Ops, SparseCore 0:
  9.6 60.9 all-gather.4
